TPU v7x, 32 devices: a whole 2x2x4 slice. The times are simulated.
32 devices in a mesh: band: 8 (over y, x, core), ga: 4 (over z).
Axes of the slice: x: 2, y: 2, z: 4, core: 2. Of those that a mesh axis runs over, the one named last changes fastest.
Arguments:
- orbitals: bfloat16 [256, 90112], P(('band', 'ga')), may hold values from -6 to 6
- local_part: bfloat16 [256, 90112], P(('band', 'ga')), may hold values from -6 to 6
- projectors: bfloat16 [90112, 1664], P(('band', 'ga')), may hold values from -0.01953125 to 0.01953125
- couplings: float32 [4, 13, 13], replicated, may hold values from -20 to 20, as said below
- species: int32 [128], replicated, may hold values from 0 to 3
Outputs:
- applied: bfloat16 [256, 90112], P(('band', 'ga'))
Inputs may be any that keep to these rules, and one draw needn't show every extreme that they name: `couplings`: each species has one symmetric block.
All inputs are finite; a program needn't handle non-finite values.
Results may differ from a plain program's by a relative error of at most 0.0056.
Values may be sent and summed in bfloat16 or wider, within the bound.
A program may use at most 64 MiB of HBM per device.

v0:
```python
import jax
import jax.numpy as jnp
from jax import lax
from jax.sharding import PartitionSpec as P


def select_blocks(couplings, species):
    kinds = couplings.shape[0]
    width = couplings.shape[1]
    select = (jnp.arange(kinds, dtype=jnp.int32)[:, None] == species[None, :]).astype(jnp.float32)
    table = jnp.einsum(
        "sk,sa->ka",
        couplings.reshape(kinds, width * width),
        select,
        precision=lax.Precision.HIGHEST,
    )
    return table.reshape(width, width, species.shape[0])


def couple(totals, blocks):
    width = blocks.shape[0]
    atom_count = blocks.shape[2]
    folded = totals.reshape(totals.shape[0], width, atom_count)
    mixed = jnp.zeros_like(folded)
    for inner in range(width):
        mixed = mixed + folded[:, inner, None, :] * blocks[None, inner, :, :]
    return mixed.reshape(totals.shape[0], width * atom_count).astype(jnp.bfloat16)


def expand(coefs, projectors):
    return jnp.einsum("bp,gp->bg", coefs, projectors, preferred_element_type=jnp.float32).astype(
        jnp.bfloat16
    )


def on_device(orbitals, local_part, projectors, couplings, species):
    blocks = select_blocks(couplings, species)
    slab_orbitals = lax.all_to_all(
        orbitals, ("band", "ga"), split_axis=1, concat_axis=0, tiled=True
    )
    partial_value = jnp.dot(slab_orbitals, projectors, preferred_element_type=jnp.float32)
    devices = lax.axis_size(("band", "ga"))
    pieces = lax.all_to_all(
        partial_value.astype(jnp.bfloat16), ("band", "ga"), split_axis=0, concat_axis=0, tiled=True
    )
    pieces = pieces.reshape(devices, pieces.shape[0] // devices, pieces.shape[1])
    totals = jnp.sum(pieces.astype(jnp.float32), axis=0)
    coefs = lax.all_gather(couple(totals, blocks), ("band", "ga"), axis=0, tiled=True)
    slab_correction = expand(coefs, projectors)
    correction = lax.all_to_all(
        slab_correction, ("band", "ga"), split_axis=0, concat_axis=1, tiled=True
    )
    correction = lax.optimization_barrier(correction)
    return (local_part.astype(jnp.float32) + correction.astype(jnp.float32)).astype(jnp.bfloat16)


def solution(mesh):
    placed = (P(("band", "ga"), None), P(("band", "ga"), None), P(("band", "ga"), None), P(), P())
    return jax.shard_map(
        on_device, mesh=mesh, in_specs=placed, out_specs=P(("band", "ga"), None), check_vma=False
    )
```

profile of v0, /device:TPU:1, one launch (start us, length us, event | category | flops | bytes accessed | tf_op | source)
XLA Modules:
  0.0 192.5 jit_solution(15892471655889466248)
XLA Ops:
  0.0 42.4 %all_to_all.47 = bf16[8,32,2816]{2,0,1:T(8,128)(2,1)S(1)} all-to-all(bf16[8,32,2816]{2,0,1:T(8,128)(2,1)} %bitcast.149), channel_id=1, replica_groups=mesh['band'=8,'ga'=4] {'band','ga'}, dimensions={1} | all-to-all | bytes 2883584 | tf_op jit(solution)/shard_map/all_to_all | solution.py:38
  42.4 7.3 %fusion.1 = bf16[32,8,1664]{2,1,0:T(8,128)(2,1)} fusion(bf16[2816,1664]{1,0:T(8,128)(2,1)} %param.7, bf16[8,32,2816]{2,0,1:T(8,128)(2,1)S(1)} %all_to_all.47), kind=kOutput, calls=%fused_computation.4 | convolution fusion | flops 2399567872 | bytes 11665408 | tf_op jit(solution)/shard_map/dot_general | solution.py:41
  49.7 0.0 copy-start.1
  49.7 0.0 copy-start.2
  49.7 2.8 %all-to-all-start.1 = ((bf16[32,8,1664]{2,1,0:T(8,128)(2,1)}), bf16[32,8,1664]{2,1,0:T(8,128)(2,1)S(1)}, u32[]{:S(2)}, u32[]{:S(2)}) async-start(bf16[32,8,1664]{2,1,0:T(8,128)(2,1)} %fusion.1), calls=%async_computation.1 | async-start | bytes 1703936 | tf_op jit(solution)/shard_map/all_to_all | solution.py:43
  52.6 0.0 copy-done.1
  52.6 0.1 reshape.85
  52.7 0.0 copy-done.2
  52.7 0.3 convolution_bitcast_fusion
  53.0 21.8 %all-to-all-done.1 = bf16[32,8,1664]{2,1,0:T(8,128)(2,1)S(1)} async-done(((bf16[32,8,1664]{2,1,0:T(8,128)(2,1)}), bf16[32,8,1664]{2,1,0:T(8,128)(2,1)S(1)}, u32[]{:S(2)}, u32[]{:S(2)}) %all-to-all-start.1) | async-done | bytes 852000 | tf_op jit(solution)/shard_map/all_to_all | solution.py:43
  74.8 0.1 convert_reduce_fusion
  74.9 0.1 fusion.4
  75.0 67.2 %all_gather.3 = bf16[256,1664]{1,0:T(8,128)(2,1)S(1)} all-gather(bf16[8,1664]{1,0:T(8,128)(2,1)S(1)} %fusion.4), channel_id=1, replica_groups=mesh['band'=8,'ga'=4] {'band','ga'}, dimensions={0}, use_global_device_ids=true | all-gather | bytes 878592 | tf_op jit(solution)/shard_map/all_gather | solution.py:48
  142.2 6.5 %fusion = bf16[32,8,2816]{2,1,0:T(8,128)(2,1)S(1)} fusion(bf16[256,1664]{1,0:T(8,128)(2,1)S(1)} %all_gather.3, bf16[2816,1664]{1,0:T(8,128)(2,1)} %param.7), kind=kOutput, calls=%fused_computation.1 | convolution fusion | flops 2399862784 | bytes 11665408 | tf_op jit(solution)/shard_map/bp,gp->bg/dot_general | solution.py:31
  148.7 0.0 copy-start
  148.7 42.4 %all_to_all.48 = bf16[32,8,2816]{2,1,0:T(8,128)(2,1)S(1)} all-to-all(bf16[32,8,2816]{2,1,0:T(8,128)(2,1)S(1)} %fusion), channel_id=1, replica_groups=mesh['band'=8,'ga'=4] {'band','ga'}, dimensions={0} | all-to-all | bytes 2883584 | tf_op jit(solution)/shard_map/all_to_all | solution.py:50
  191.1 0.0 copy-done
  191.1 1.4 add_convert_fusion
  (3 shorter events, 0.0 us)
Async XLA Ops:
  49.7 2.9 %copy-start.1 = (f32[4,13,13]{2,0,1:T(4,128)S(1)}, f32[4,13,13]{2,0,1:T(4,128)}, u32[]{:S(2)}) copy-start(f32[4,13,13]{2,0,1:T(4,128)} %param.8) | copy-start | bytes 8116
  49.7 3.0 %copy-start.2 = (s32[128]{0:T(128)S(1)}, s32[128]{0:T(128)}, u32[]{:S(2)}) copy-start(s32[128]{0:T(128)} %param.9) | copy-start | bytes 1540
  49.7 25.0 %all-to-all-start.1 = ((bf16[32,8,1664]{2,1,0:T(8,128)(2,1)}), bf16[32,8,1664]{2,1,0:T(8,128)(2,1)S(1)}, u32[]{:S(2)}, u32[]{:S(2)}) async-start(bf16[32,8,1664]{2,1,0:T(8,128)(2,1)} %fusion.1), calls=%async_computation.1 | async-start | bytes 1703936 | tf_op jit(solution)/shard_map/all_to_all | solution.py:43
  148.7 42.4 %copy-start = (bf16[8,90112]{1,0:T(8,128)(2,1)S(1)}, bf16[8,90112]{1,0:T(8,128)(2,1)}, u32[]{:S(2)}) copy-start(bf16[8,90112]{1,0:T(8,128)(2,1)} %param.6) | copy-start | bytes 4325380
where the time goes:
time: 193 us
  blocking collectives  152 us (79%)
  waiting for transfers between devices  21.8 us (11%)
  matrix products  14.1 us (7%)
  starting transfers between devices  2.84 us (1%)
    all_gather x1, blocking collectives, on_device(): lax.all_gather(couple(totals, blocks), ('band', 'ga'), axis=0, tiled=True)  67.2 us
    all_to_all x1, blocking collectives, on_device(): lax.all_to_all(slab_correction, ('band', 'ga'), split_axis=0, concat_axis...  42.4 us
    all_to_all x1, blocking collectives, on_device(): lax.all_to_all(orbitals, ('band', 'ga'), split_axis=1, concat_axis=0, til...  42.4 us
    all_to_all x1, waiting for transfers between devices, on_device(): lax.all_to_all(partial_value.astype(jnp.bfloat16), ('band', 'ga'), split_...  21.8 us
    dot_general x1, matrix products, on_device(): jnp.dot(slab_orbitals, projectors, preferred_element_type=jnp.float32)  7.35 us
    dot_general x1, matrix products, expand(): jnp.einsum('bp,gp->bg', coefs, projectors, preferred_element_type=jnp.flo...  6.5 us
  transfers between devices with their start and end apart: 1, of which 1 were waited for; matrix products, arithmetic and copies ran while one was open for 0% of the time, Pallas kernels for 0%

commit v1 on v0

--- a/solution.py
+++ b/solution.py
@@ -47,9 +47,9 @@
     totals = jnp.sum(pieces.astype(jnp.float32), axis=0)
     coefs = lax.all_gather(couple(totals, blocks), ("band", "ga"), axis=0, tiled=True)
     slab_correction = expand(coefs, projectors)
-    correction = lax.all_to_all(
-        slab_correction, ("band", "ga"), split_axis=0, concat_axis=1, tiled=True
-    )
+    cells = jnp.split(slab_correction, lax.axis_size(("band", "ga")), axis=0)
+    received = lax.all_to_all(jnp.stack(cells), ("band", "ga"), 0, 0)
+    correction = jnp.concatenate(received, axis=1)
     correction = lax.optimization_barrier(correction)
     return (local_part.astype(jnp.float32) + correction.astype(jnp.float32)).astype(jnp.bfloat16)
 

time: 193 us -> 193 us (level)
  no operation moved by 1% of the time
where the time goes in v1:
time: 193 us
  blocking collectives  152 us (79%)
  waiting for transfers between devices  21.8 us (11%)
  matrix products  14.1 us (7%)
  starting transfers between devices  2.84 us (1%)
    all_gather x1, blocking collectives, on_device(): lax.all_gather(couple(totals, blocks), ('band', 'ga'), axis=0, tiled=True)  67.2 us
    all_to_all x1, blocking collectives, on_device(): received = lax.all_to_all(jnp.stack(cells), ('band', 'ga'), 0, 0)  42.4 us
    all_to_all x1, blocking collectives, on_device(): lax.all_to_all(orbitals, ('band', 'ga'), split_axis=1, concat_axis=0, til...  42.4 us
    all_to_all x1, waiting for transfers between devices, on_device(): lax.all_to_all(partial_value.astype(jnp.bfloat16), ('band', 'ga'), split_...  21.8 us
    dot_general x1, matrix products, on_device(): jnp.dot(slab_orbitals, projectors, preferred_element_type=jnp.float32)  7.35 us
    dot_general x1, matrix products, expand(): jnp.einsum('bp,gp->bg', coefs, projectors, preferred_element_type=jnp.flo...  6.46 us
  transfers between devices with their start and end apart: 1, of which 1 were waited for; matrix products, arithmetic and copies ran while one was open for 0% of the time, Pallas kernels for 0%

profile of v1, /device:TPU:1, one launch (start us, length us, event | category | flops | bytes accessed | tf_op | source)
XLA Modules:
  0.0 192.9 jit_solution(10892091289672235637)
XLA Ops:
  0.0 42.4 %all_to_all.33 = bf16[8,32,2816]{2,0,1:T(8,128)(2,1)S(1)} all-to-all(bf16[8,32,2816]{2,0,1:T(8,128)(2,1)} %bitcast.275), channel_id=1, replica_groups=mesh['band'=8,'ga'=4] {'band','ga'}, dimensions={1} | all-to-all | bytes 2883584 | tf_op jit(solution)/shard_map/all_to_all | solution.py:38
  42.4 7.3 %fusion = bf16[32,8,1664]{2,1,0:T(8,128)(2,1)} fusion(bf16[2816,1664]{1,0:T(8,128)(2,1)} %param.7, bf16[8,32,2816]{2,0,1:T(8,128)(2,1)S(1)} %all_to_all.33), kind=kOutput, calls=%fused_computation.3 | convolution fusion | flops 2399567872 | bytes 11665408 | tf_op jit(solution)/shard_map/dot_general | solution.py:41
  49.7 0.0 copy-start.1
  49.7 0.0 copy-start.2
  49.7 2.8 %all-to-all-start.1 = ((bf16[32,8,1664]{2,1,0:T(8,128)(2,1)}), bf16[32,8,1664]{2,1,0:T(8,128)(2,1)S(1)}, u32[]{:S(2)}, u32[]{:S(2)}) async-start(bf16[32,8,1664]{2,1,0:T(8,128)(2,1)} %fusion), calls=%async_computation.1 | async-start | bytes 1703936 | tf_op jit(solution)/shard_map/all_to_all | solution.py:43
  52.6 0.0 copy-done.1
  52.6 0.1 reshape.88
  52.7 0.0 copy-done.2
  52.7 0.3 convolution_bitcast_fusion
  53.0 21.8 %all-to-all-done.1 = bf16[32,8,1664]{2,1,0:T(8,128)(2,1)S(1)} async-done(((bf16[32,8,1664]{2,1,0:T(8,128)(2,1)}), bf16[32,8,1664]{2,1,0:T(8,128)(2,1)S(1)}, u32[]{:S(2)}, u32[]{:S(2)}) %all-to-all-start.1) | async-done | bytes 852000 | tf_op jit(solution)/shard_map/all_to_all | solution.py:43
  74.8 0.1 convert_reduce_fusion
  74.9 0.1 fusion.3
  75.0 67.2 %all_gather.3 = bf16[256,1664]{1,0:T(8,128)(2,1)S(1)} all-gather(bf16[8,1664]{1,0:T(8,128)(2,1)S(1)} %fusion.3), channel_id=1, replica_groups=mesh['band'=8,'ga'=4] {'band','ga'}, dimensions={0}, use_global_device_ids=true | all-gather | bytes 878592 | tf_op jit(solution)/shard_map/all_gather | solution.py:48
  142.2 6.5 %convolution_convert_fusion = bf16[256,2816]{1,0:T(8,128)(2,1)S(1)} fusion(bf16[256,1664]{1,0:T(8,128)(2,1)S(1)} %all_gather.3, bf16[2816,1664]{1,0:T(8,128)(2,1)} %param.7), kind=kOutput, calls=%fused_computation | convolution fusion | flops 2399862784 | bytes 11665408 | tf_op jit(solution)/shard_map/bp,gp->bg/dot_general | solution.py:31
  149.1 0.0 copy-start
  149.1 42.4 %all_to_all.34 = bf16[32,8,2816]{2,1,0:T(8,128)(2,1)S(1)} all-to-all(bf16[32,8,2816]{2,1,0:T(8,128)(2,1)S(1)} %constant_dynamic-update-slice_fusion), channel_id=1, replica_groups=mesh['band'=8,'ga'=4] {'band','ga'}, dimensions={0} | all-to-all | bytes 2883584 | tf_op jit(solution)/shard_map/all_to_all | solution.py:51
  191.5 0.0 copy-done
  191.5 1.4 add_convert_fusion
  (35 shorter events, 0.2 us)
Async XLA Ops:
  49.7 2.9 %copy-start.1 = (f32[4,13,13]{2,0,1:T(4,128)S(1)}, f32[4,13,13]{2,0,1:T(4,128)}, u32[]{:S(2)}) copy-start(f32[4,13,13]{2,0,1:T(4,128)} %param.8) | copy-start | bytes 8116
  49.7 3.0 %copy-start.2 = (s32[128]{0:T(128)S(1)}, s32[128]{0:T(128)}, u32[]{:S(2)}) copy-start(s32[128]{0:T(128)} %param.9) | copy-start | bytes 1540
  49.7 25.0 %all-to-all-start.1 = ((bf16[32,8,1664]{2,1,0:T(8,128)(2,1)}), bf16[32,8,1664]{2,1,0:T(8,128)(2,1)S(1)}, u32[]{:S(2)}, u32[]{:S(2)}) async-start(bf16[32,8,1664]{2,1,0:T(8,128)(2,1)} %fusion), calls=%async_computation.1 | async-start | bytes 1703936 | tf_op jit(solution)/shard_map/all_to_all | solution.py:43
  149.1 42.4 %copy-start = (bf16[8,90112]{1,0:T(8,128)(2,1)S(1)}, bf16[8,90112]{1,0:T(8,128)(2,1)}, u32[]{:S(2)}) copy-start(bf16[8,90112]{1,0:T(8,128)(2,1)} %param.6) | copy-start | bytes 4325380
